TPU v7x, 32 devices: a whole 2x2x4 slice. The times are simulated.
32 devices in a mesh: expert: 8 (over y, x, core), hidden: 4 (over z).
Axes of the slice: x: 2, y: 2, z: 4, core: 2. Of those that a mesh axis runs over, the one named last changes fastest.
Arguments:
- weight: bfloat16 [8, 1536, 4096], P('expert', 'hidden'), may hold values from -0.15625 to 0.15625
- scales: float32 [8, 12, 32], P('expert'), may hold values from 0.5 to 2
- act_own: bfloat16 [8, 128, 1536], P('expert', None, 'hidden'), may hold values from -6 to 6
- dy_own: bfloat16 [8, 128, 4096], P('expert'), may hold values from -6 to 6
- own_count: int32 [8], P('expert'), may hold values from 1 to 128, as said below
- act_help: bfloat16 [8, 32, 1536], P('expert', None, 'hidden'), may hold values from -6 to 6
- dy_help: bfloat16 [8, 32, 4096], P('expert'), may hold values from -6 to 6
- help_count: int32 [8], P('expert'), may hold values from 1 to 32, as said below
- hot: int32 [1], replicated, may hold values from 0 to 7
Outputs:
- y_own: bfloat16 [8, 128, 4096], P('expert', None, 'hidden')
- dact_own: bfloat16 [8, 128, 1536], P('expert', None, 'hidden')
- own_grad: bfloat16 [8, 1536, 4096], P('expert', 'hidden')
- y_help: bfloat16 [8, 32, 4096], P('expert', None, 'hidden')
- dact_help: bfloat16 [8, 32, 1536], P('expert', None, 'hidden')
- hot_grad: float32 [1536, 4096], P('hidden', 'expert')
Inputs may be any that keep to these rules, and one draw needn't show every extreme that they name: `own_count`: some expert has exactly 128 live rows. `help_count`: some group has exactly 32 live rows.
All inputs are finite; a program needn't handle non-finite values.
Results may differ from a plain program's by a relative error of at most 0.013.
Values may be sent and summed in bfloat16 or wider, within the bound.
No kernel may reach another device: no remote copies, remote signals or barrier semaphores. Data moves between devices by JAX's collectives and lax.ppermute only.
A program may use at most 64 MiB of HBM per device.

v0:
```python
import jax
import jax.numpy as jnp
from jax import lax
from jax.sharding import PartitionSpec as P

block_edge = 128


def from_root(block, axis, source):
    block = jnp.where(lax.axis_index(axis) == source, block, jnp.zeros_like(block))
    return lax.psum(block, axis)


def dequant(weight, scales, slice_start):
    height = weight.shape[1]
    depth = weight.shape[2]
    blocks = (slice_start + jnp.arange(height, dtype=jnp.int32)) // block_edge
    select = (blocks[:, None] == jnp.arange(scales.shape[1], dtype=jnp.int32)[None, :]).astype(
        jnp.float32
    )
    row_scale = jnp.einsum("fb,ebc->efc", select, scales, precision=lax.Precision.HIGHEST)
    shaped = weight.reshape(weight.shape[0], height, depth // block_edge, block_edge).astype(
        jnp.float32
    )
    shaped = shaped * row_scale[..., None]
    return shaped.reshape(weight.shape).astype(jnp.bfloat16)


def masked(values, count):
    live = jnp.arange(values.shape[1], dtype=jnp.int32)[None, :, None] < count[:, None, None]
    return jnp.where(live, values, jnp.zeros_like(values))


def body(weight, scales, act_own, dy_own, own_count, act_help, dy_help, help_count, hot):
    slice_start = lax.axis_index("hidden") * weight.shape[1]
    own_weight = dequant(weight, scales, slice_start)
    experts_here = weight.shape[0]
    hot_index = hot[0]
    hot_local = hot_index % experts_here
    hot_root = hot_index // experts_here
    own_rows = masked(act_own, own_count)
    own_grads = masked(dy_own, own_count)
    help_rows = masked(act_help, help_count)[0]
    help_grads = masked(dy_help, help_count)[0]
    partial_value = jnp.einsum(
        "erf,efd->erd", own_rows, own_weight, preferred_element_type=jnp.float32
    )
    dact = jnp.einsum("erd,efd->erf", own_grads, own_weight, preferred_element_type=jnp.float32)
    gradient = jnp.einsum("erf,erd->efd", own_rows, own_grads, preferred_element_type=jnp.float32)
    dact_own = dact.astype(jnp.bfloat16)
    own_grad = gradient.astype(jnp.bfloat16)
    chosen = lax.dynamic_index_in_dim(own_weight, hot_local, 0, keepdims=False)
    hot_weight = from_root(chosen, "expert", hot_root)
    help_partial_value = jnp.dot(help_rows, hot_weight, preferred_element_type=jnp.float32)
    dact = lax.dot_general(
        help_grads, hot_weight, (((1,), (1,)), ((), ())), preferred_element_type=jnp.float32
    )
    gradient = lax.dot_general(
        help_rows, help_grads, (((0,), (0,)), ((), ())), preferred_element_type=jnp.float32
    )
    summed = lax.psum_scatter(gradient, "expert", scatter_dimension=1, tiled=True)
    help_partial = help_partial_value[None]
    dact_help = dact.astype(jnp.bfloat16)[None]
    y_own, y_help = (
        lax.psum_scatter(
            partial_value.astype(jnp.bfloat16), "hidden", scatter_dimension=2, tiled=True
        ).astype(jnp.float32),
        lax.psum_scatter(
            help_partial.astype(jnp.bfloat16), "hidden", scatter_dimension=2, tiled=True
        ).astype(jnp.float32),
    )
    return (
        y_own.astype(jnp.bfloat16),
        dact_own,
        own_grad,
        y_help.astype(jnp.bfloat16),
        dact_help,
        summed,
    )


def solution(mesh):
    return jax.shard_map(
        body,
        mesh=mesh,
        in_specs=(
            P("expert", "hidden", None),
            P("expert", None, None),
            P("expert", None, "hidden"),
            P("expert", None, None),
            P("expert"),
            P("expert", None, "hidden"),
            P("expert", None, None),
            P("expert"),
            P(),
        ),
        out_specs=(
            P("expert", None, "hidden"),
            P("expert", None, "hidden"),
            P("expert", "hidden", None),
            P("expert", None, "hidden"),
            P("expert", None, "hidden"),
            P("hidden", "expert"),
        ),
        check_vma=False,
    )
```

profile of v0, /device:TPU:0, one launch (start us, length us, event | category | flops | bytes accessed | tf_op | source)
XLA Modules:
  0.0 194.3 jit_solution(13138229122066029622)
XLA Ops:
  8.0 0.0 all-reduce.2.cloned.1.call-start
  8.1 1.0 fusion.11
  9.1 3.8 %mul.18 = f32[384,32,128]{2,1,0:T(8,128)} broadcast(f32[384,32]{1,0:T(8,128)S(1)} %fusion.11), dimensions={0,1} | broadcast | bytes 6340608 | tf_op jit(solution)/shard_map/mul | solution.py:25
  12.9 7.2 %mul.19 = f32[1,384,4096]{2,1,0:T(8,128)} reshape(f32[384,32,128]{2,1,0:T(8,128)} %mul.18) | data formatting | bytes 12582912 | tf_op jit(solution)/shard_map/mul | solution.py:25
  20.7 6.8 %broadcast_select_fusion = (bf16[384,4096]{1,0:T(8,128)(2,1)}, bf16[384,4096]{1,0:T(8,128)(2,1)S(1)}) fusion(pred[]{:T(512)S(6)} %eq.21, f32[1,384,4096]{2,1,0:T(8,128)} %mul.19, bf16[1,384,4096]{2,1,0:T(8,128)(2,1)} %param.9), kind=kLoop, calls=%fused_computation.8 | loop fusion | flops 6291456 | bytes 15728641 | tf_op jit(solution)/shard_map/jit(_where)/select_n | solution.py:10
  27.5 0.0 copy-start.3
  27.5 0.0 all-reduce.2.cloned.1.call-update
  27.6 0.0 copy-start.4
  27.6 0.0 reduce-scatter.4.cloned.1.call-start
  28.3 0.1 copy-done.3
  28.4 1.7 fusion.1
  30.1 0.0 copy-start.2
  30.1 0.0 reduce-scatter.4.cloned.1.call-update
  30.2 0.0 reduce-scatter.6.cloned.1.call-start
  30.9 68.8 %all-reduce.2.cloned.1.call-done = bf16[384,4096]{1,0:T(8,128)(2,1)} async-done(((bf16[384,4096]{1,0:T(8,128)(2,1)}), bf16[384,4096]{1,0:T(8,128)(2,1)}) %all-reduce.2.cloned.1.call-update) | async-done | bytes 3145744 | tf_op jit(solution)/shard_map/psum | solution.py:11
  99.7 0.0 copy-done.4
  99.7 3.3 %fusion.2 = bf16[1,32,4096]{2,1,0:T(8,128)(2,1)} fusion(bf16[384,4096]{1,0:T(8,128)(2,1)} %all-reduce.2.cloned.1.call-done, bf16[1,32,384]{2,1,0:T(8,128)(2,1)S(1)} %copy-done.4, pred[32]{0:T(512)(128)(4,1)S(1)} %iota_compare_fusion.2), kind=kOutput, calls=%fused_computation.6 | convolution fusion | flops 100806656 | bytes 3432480 | tf_op jit(solution)/shard_map/dot_general | solution.py:54
  103.0 0.0 reduce-scatter.6.cloned.1.call-update
  103.1 0.0 reduce-scatter.8.cloned.1.call-start
  103.1 0.0 copy-done.2
  103.1 3.7 %fusion.8 = f32[384,4096]{1,0:T(8,128)} fusion(bf16[1,32,4096]{2,1,0:T(8,128)(2,1)S(1)} %copy-done.2, pred[32]{0:T(512)(128)(4,1)S(1)} %iota_compare_fusion.2, bf16[1,32,384]{2,1,0:T(8,128)(2,1)S(1)} %copy-done.4), kind=kOutput, calls=%fused_computation.16 | convolution fusion | flops 100806656 | bytes 6578208 | tf_op jit(solution)/shard_map/dot_general | solution.py:58
  106.8 0.0 reduce-scatter.8.cloned.1.call-update
  106.9 0.0 copy-start.1
  106.9 4.1 %fusion = bf16[1,384,4096]{2,1,0:T(8,128)(2,1)} fusion(bf16[1,128,4096]{2,1,0:T(8,128)(2,1)} %param.12, pred[128]{0:T(512)(128)(4,1)S(1)} %iota_compare_fusion.3, bf16[1,128,384]{2,1,0:T(8,128)(2,1)S(1)} %copy-done.3), kind=kOutput, calls=%fused_computation.2 | convolution fusion | flops 404799488 | bytes 4292736 | tf_op jit(solution)/shard_map/erf,erd->efd/dot_general | solution.py:49
  110.9 0.0 copy-done.1
  110.9 0.0 copy-start
  110.9 1.7 fusion.4
  112.7 0.2 copy-done
  112.8 1.7 fusion.5
  114.5 0.0 reduce-scatter.4.cloned.1.call-done
  114.5 8.7 %reduce-scatter.6.cloned.1.call-done = bf16[1,32,1024]{2,1,0:T(8,128)(2,1)} async-done(((bf16[1,32,4096]{2,1,0:T(8,128)(2,1)}), bf16[1,32,1024]{2,1,0:T(8,128)(2,1)}) %reduce-scatter.6.cloned.1.call-update) | async-done | bytes 65552 | tf_op jit(solution)/shard_map/reduce_scatter | solution.py:68
  123.2 63.6 %reduce-scatter.8.cloned.1.call-done = f32[384,512]{1,0:T(8,128)} async-done(((f32[384,4096]{1,0:T(8,128)}), f32[384,512]{1,0:T(8,128)}) %reduce-scatter.8.cloned.1.call-update) | async-done | bytes 786448 | tf_op jit(solution)/shard_map/reduce_scatter | solution.py:61
  (3 shorter events, 0.0 us)
Async XLA Ops:
  8.0 91.7 %all-reduce.2.cloned.1.call-start = ((), (), s32[]{:S(2)}) async-start(), calls=%async_computation.4 | async-start | bytes 6291456 | tf_op jit(solution)/shard_map/psum | solution.py:11
  27.5 0.9 copy-start.3
  27.6 72.2 %copy-start.4 = (bf16[1,32,384]{2,1,0:T(8,128)(2,1)S(1)}, bf16[1,32,384]{2,1,0:T(8,128)(2,1)}, u32[]{:S(2)}) copy-start(bf16[1,32,384]{2,1,0:T(8,128)(2,1)} %param.14) | copy-start | bytes 73732
  27.6 86.9 %reduce-scatter.4.cloned.1.call-start = ((), (), s32[]{:S(2)}) async-start(), calls=%async_computation.3 | async-start | bytes 1310720 | tf_op jit(solution)/shard_map/reduce_scatter | solution.py:65
  30.1 73.0 %copy-start.2 = (bf16[1,32,4096]{2,1,0:T(8,128)(2,1)S(1)}, bf16[1,32,4096]{2,1,0:T(8,128)(2,1)}, u32[]{:S(2)}) copy-start(bf16[1,32,4096]{2,1,0:T(8,128)(2,1)} %param.15) | copy-start | bytes 786436
  30.2 93.0 %reduce-scatter.6.cloned.1.call-start = ((), (), s32[]{:S(2)}) async-start(), calls=%async_computation.5 | async-start | bytes 327680 | tf_op jit(solution)/shard_map/reduce_scatter | solution.py:68
  103.1 83.7 %reduce-scatter.8.cloned.1.call-start = ((), (), s32[]{:S(2)}) async-start(), calls=%async_computation.6 | async-start | bytes 7077888 | tf_op jit(solution)/shard_map/reduce_scatter | solution.py:61
  106.9 4.1 %copy-start.1 = (bf16[1,128,4096]{2,1,0:T(8,128)(2,1)S(1)}, bf16[1,128,4096]{2,1,0:T(8,128)(2,1)}, u32[]{:S(2)}) copy-start(bf16[1,128,4096]{2,1,0:T(8,128)(2,1)} %param.12) | copy-start | bytes 3145732
  110.9 1.9 copy-start
Sparse Core Ops, SparseCore 0:
  27.7 72.0 all-reduce.1
Sparse Core Ops, SparseCore 1:
  30.9 29.9 reduce-scatter.3
  103.1 20.0 reduce-scatter.5
  127.0 59.7 reduce-scatter.7
where the time goes:
time: 195 us; the launch traced here: 194 us
  waiting for transfers between devices  141 us (72%)
  between operations  17.7 us (9%)
  matrix products  17.2 us (9%)
  local copies, waits for them, and re-layouts  11.3 us (6%)
  other arithmetic  6.87 us (4%)
    psum x1, waiting for transfers between devices, from_root(): return lax.psum(block, axis)  68.8 us
    reduce_scatter x1, waiting for transfers between devices, body(): lax.psum_scatter(gradient, 'expert', scatter_dimension=1, tiled=True)  63.6 us
    mul x2, local copies, waits for them, and re-layouts, dequant(): shaped = shaped * row_scale[..., None]  11 us
    reduce_scatter x1, waiting for transfers between devices, body(): lax.psum_scatter(help_partial.astype(jnp.bfloat16), 'hidden', scatter_dim...  8.65 us
    select_n x1, other arithmetic, from_root(): jnp.where(lax.axis_index(axis) == source, block, jnp.zeros_like(block))  6.85 us
    dot_general x1, matrix products, body(): jnp.einsum('erf,erd->efd', own_rows, own_grads, preferred_element_type=jn...  4.06 us
  transfers between devices with their start and end apart: 4, of which 3 were waited for; matrix products, arithmetic and copies ran while one was open for 8% of the time, Pallas kernels for 0%

commit v1 on v0

--- a/solution.py
+++ b/solution.py
@@ -8,7 +8,7 @@
 
 def from_root(block, axis, source):
     block = jnp.where(lax.axis_index(axis) == source, block, jnp.zeros_like(block))
-    return lax.psum(block, axis)
+    return jnp.sum(lax.all_gather(block, axis), axis=0)
 
 
 def dequant(weight, scales, slice_start):

time: 195 us -> 219 us (1.12)
  other arithmetic: 6.87 us -> 20.4 us
  waiting for transfers between devices: 141 us -> 152 us
    all_gather x0 -> x1, waiting for transfers between devices: none -> 121 us  [from_root(): return jnp.sum(lax.all_gather(block, axis), axis=0)]
    psum x1 -> x0, waiting for transfers between devices: 68.8 us -> none  [from_root(): return lax.psum(block, axis)]
    reduce_scatter x1, waiting for transfers between devices: 63.6 us -> 8.9 us  [body(): lax.psum_scatter(gradient, 'expert', scatter_dimension=1, tiled=True)]
    reduce_scatter x1, waiting for transfers between devices: 8.65 us -> 22.6 us  [body(): lax.psum_scatter(help_partial.astype(jnp.bfloat16), 'hidden', scatter_dim...]
    reduce_sum x0 -> x1, other arithmetic: none -> 13.5 us  [from_root(): return jnp.sum(lax.all_gather(block, axis), axis=0)]
    dot_general x1, matrix products: 1.71 us -> 4.01 us  [body(): jnp.einsum('erd,efd->erf', own_grads, own_weight, preferred_element_type=...]
  transfers between devices with their start and end apart: 4 -> 4, of which waited for: 3 -> 3; matrix products, arithmetic and copies ran while one was open for 8% -> 13% of each run, Pallas kernels for 0% -> 0%
where the time goes in v1:
time: 219 us; the launch traced here: 218 us
  waiting for transfers between devices  152 us (69%)
  other arithmetic  20.4 us (9%)
  between operations  18.1 us (8%)
  matrix products  16.4 us (7%)
  local copies, waits for them, and re-layouts  11 us (5%)
    all_gather x1, waiting for transfers between devices, from_root(): return jnp.sum(lax.all_gather(block, axis), axis=0)  121 us
    reduce_scatter x1, waiting for transfers between devices, body(): lax.psum_scatter(help_partial.astype(jnp.bfloat16), 'hidden', scatter_dim...  22.6 us
    reduce_sum x1, other arithmetic, from_root(): return jnp.sum(lax.all_gather(block, axis), axis=0)  13.5 us
    mul x2, local copies, waits for them, and re-layouts, dequant(): shaped = shaped * row_scale[..., None]  11 us
    reduce_scatter x1, waiting for transfers between devices, body(): lax.psum_scatter(gradient, 'expert', scatter_dimension=1, tiled=True)  8.9 us
    select_n x1, other arithmetic, from_root(): jnp.where(lax.axis_index(axis) == source, block, jnp.zeros_like(block))  6.85 us
  transfers between devices with their start and end apart: 4, of which 3 were waited for; matrix products, arithmetic and copies ran while one was open for 13% of the time, Pallas kernels for 0%

profile of v1, /device:TPU:0, one launch (start us, length us, event | category | flops | bytes accessed | tf_op | source)
XLA Modules:
  0.0 218.5 jit_solution(1845318768002982627)
XLA Ops:
  8.0 0.0 all-gather.2.cloned.1.call-start
  8.1 1.0 fusion.18
  9.1 3.8 %mul.18 = f32[384,32,128]{2,1,0:T(8,128)} broadcast(f32[384,32]{1,0:T(8,128)S(1)} %fusion.18), dimensions={0,1} | broadcast | bytes 6340608 | tf_op jit(solution)/shard_map/mul | solution.py:25
  12.9 7.2 %mul.19 = f32[1,384,4096]{2,1,0:T(8,128)} reshape(f32[384,32,128]{2,1,0:T(8,128)} %mul.18) | data formatting | bytes 12582912 | tf_op jit(solution)/shard_map/mul | solution.py:25
  20.7 6.8 %broadcast_select_fusion = (bf16[1,384,4096]{2,1,0:T(8,128)(2,1)}, bf16[1,384,4096]{2,1,0:T(8,128)(2,1)S(1)}) fusion(pred[]{:T(512)S(6)} %eq.21, f32[1,384,4096]{2,1,0:T(8,128)} %mul.19, bf16[1,384,4096]{2,1,0:T(8,128)(2,1)} %param.9), kind=kLoop, calls=%fused_computation.10 | loop fusion | flops 6291456 | bytes 15728641 | tf_op jit(solution)/shard_map/jit(_where)/select_n | solution.py:10
  27.5 0.0 copy-start
  27.5 0.0 copy-start.3
  27.5 0.0 all-gather.2.cloned.1.call-update
  27.6 0.0 copy-start.2
  27.6 0.0 copy-start.4
  27.6 0.0 reduce-scatter.4.cloned.1.call-start
  28.7 0.0 copy-done.3
  28.7 1.8 fusion.1
  30.5 0.0 copy-done
  30.5 0.0 reduce-scatter.4.cloned.1.call-update
  30.5 0.0 reduce-scatter.8.cloned.1.call-start
  31.2 0.0 copy-done.2
  31.2 0.0 copy-done.4
  31.2 3.8 %fusion.15 = f32[384,4096]{1,0:T(8,128)} fusion(bf16[1,32,4096]{2,1,0:T(8,128)(2,1)S(1)} %copy-done.2, pred[32]{0:T(512)(128)(4,1)S(1)} %iota_compare_fusion.2, bf16[1,32,384]{2,1,0:T(8,128)(2,1)S(1)} %copy-done.4), kind=kOutput, calls=%fused_computation.18 | convolution fusion | flops 100806656 | bytes 6578208 | tf_op jit(solution)/shard_map/dot_general | solution.py:58
  35.0 0.0 reduce-scatter.8.cloned.1.call-update
  35.0 0.0 reduce-scatter.6.cloned.1.call-start
  35.1 120.9 %all-gather.2.cloned.1.call-done = bf16[8,384,4096]{2,1,0:T(8,128)(2,1)} async-done(((bf16[1,384,4096]{2,1,0:T(8,128)(2,1)}), bf16[8,384,4096]{2,1,0:T(8,128)(2,1)}) %all-gather.2.cloned.1.call-update) | async-done | bytes 25165840 | tf_op jit(solution)/shard_map/all_gather | solution.py:11
  156.0 13.5 %reduce_sum.12 = bf16[384,4096]{1,0:T(8,128)(2,1)S(1)} reduce(bf16[8,384,4096]{2,1,0:T(8,128)(2,1)} %all-gather.2.cloned.1.call-done, bf16[]{:T(256)} %constant.47.clone.1), dimensions={0}, to_apply=%region_1.2 | reduce | flops 11010048 | bytes 28311554 | tf_op jit(solution)/shard_map/reduce_sum | solution.py:11
  169.5 1.4 fusion.2
  170.9 0.0 reduce-scatter.6.cloned.1.call-update
  170.9 0.0 copy-start.1
  170.9 4.0 %fusion.9 = bf16[1,128,384]{2,1,0:T(8,128)(2,1)} fusion(bf16[1,384,4096]{2,1,0:T(8,128)(2,1)} %copy-done, bf16[1,128,4096]{2,1,0:T(8,128)(2,1)} %param.12, pred[128]{0:T(512)(128)(4,1)S(1)} %iota_compare_fusion.3), kind=kOutput, calls=%fused_computation.12 | convolution fusion | flops 403226624 | bytes 4292736 | tf_op jit(solution)/shard_map/erd,efd->erf/dot_general | solution.py:48
  174.9 0.0 copy-done.1
  174.9 2.7 %fusion = bf16[1,384,4096]{2,1,0:T(8,128)(2,1)} fusion(bf16[1,128,4096]{2,1,0:T(8,128)(2,1)S(1)} %copy-done.1, pred[128]{0:T(512)(128)(4,1)S(1)} %iota_compare_fusion.3, bf16[1,128,384]{2,1,0:T(8,128)(2,1)S(1)} %copy-done.3), kind=kOutput, calls=%fused_computation.2 | convolution fusion | flops 404799488 | bytes 4292736 | tf_op jit(solution)/shard_map/erf,erd->efd/dot_general | solution.py:49
  177.7 1.7 fusion.12
  179.3 0.0 reduce-scatter.4.cloned.1.call-done
  179.3 8.9 %reduce-scatter.8.cloned.1.call-done = f32[384,512]{1,0:T(8,128)} async-done(((f32[384,4096]{1,0:T(8,128)}), f32[384,512]{1,0:T(8,128)}) %reduce-scatter.8.cloned.1.call-update) | async-done | bytes 786448 | tf_op jit(solution)/shard_map/reduce_scatter | solution.py:61
  188.2 22.6 %reduce-scatter.6.cloned.1.call-done = bf16[1,32,1024]{2,1,0:T(8,128)(2,1)} async-done(((bf16[1,32,4096]{2,1,0:T(8,128)(2,1)}), bf16[1,32,1024]{2,1,0:T(8,128)(2,1)}) %reduce-scatter.6.cloned.1.call-update) | async-done | bytes 65552 | tf_op jit(solution)/shard_map/reduce_scatter | solution.py:68
  (3 shorter events, 0.0 us)
Async XLA Ops:
  8.0 148.0 %all-gather.2.cloned.1.call-start = ((), (), s32[]{:S(2)}) async-start(), calls=%async_computation.4 | async-start | bytes 28311552 | tf_op jit(solution)/shard_map/all_gather | solution.py:11
  27.5 3.0 %copy-start = (bf16[1,384,4096]{2,1,0:T(8,128)(2,1)}, bf16[1,384,4096]{2,1,0:T(8,128)(2,1)S(1)}, u32[]{:S(2)}) copy-start(bf16[1,384,4096]{2,1,0:T(8,128)(2,1)S(1)} %get-tuple-element.7) | copy-start | bytes 9437188
  27.5 1.2 copy-start.3
  27.6 3.7 %copy-start.2 = (bf16[1,32,4096]{2,1,0:T(8,128)(2,1)S(1)}, bf16[1,32,4096]{2,1,0:T(8,128)(2,1)}, u32[]{:S(2)}) copy-start(bf16[1,32,4096]{2,1,0:T(8,128)(2,1)} %param.15) | copy-start | bytes 786436
  27.6 3.7 %copy-start.4 = (bf16[1,32,384]{2,1,0:T(8,128)(2,1)S(1)}, bf16[1,32,384]{2,1,0:T(8,128)(2,1)}, u32[]{:S(2)}) copy-start(bf16[1,32,384]{2,1,0:T(8,128)(2,1)} %param.14) | copy-start | bytes 73732
  27.6 151.8 %reduce-scatter.4.cloned.1.call-start = ((), (), s32[]{:S(2)}) async-start(), calls=%async_computation.3 | async-start | bytes 1310720 | tf_op jit(solution)/shard_map/reduce_scatter | solution.py:65
  30.5 157.7 %reduce-scatter.8.cloned.1.call-start = ((), (), s32[]{:S(2)}) async-start(), calls=%async_computation.6 | async-start | bytes 7077888 | tf_op jit(solution)/shard_map/reduce_scatter | solution.py:61
  35.0 175.8 %reduce-scatter.6.cloned.1.call-start = ((), (), s32[]{:S(2)}) async-start(), calls=%async_computation.5 | async-start | bytes 327680 | tf_op jit(solution)/shard_map/reduce_scatter | solution.py:68
  170.9 4.0 %copy-start.1 = (bf16[1,128,4096]{2,1,0:T(8,128)(2,1)S(1)}, bf16[1,128,4096]{2,1,0:T(8,128)(2,1)}, u32[]{:S(2)}) copy-start(bf16[1,128,4096]{2,1,0:T(8,128)(2,1)} %param.12) | copy-start | bytes 3145732
Sparse Core Ops, SparseCore 0:
  27.7 128.2 all-gather.1
Sparse Core Ops, SparseCore 1:
  30.9 29.9 reduce-scatter.3
  64.7 123.4 reduce-scatter.7
  190.9 19.9 reduce-scatter.5
